TPU v7x, 1024 devices: a whole 4x4x32 slice. The times are simulated.
1024 devices in a mesh: ctx: 128 (over z_lo, x, core), tp: 8 (over y, z_hi).
Axes of the slice: x: 4, y: 4, z: 32 (z_hi: 2, z_lo: 16; z = z_hi * 16 + z_lo), core: 2. Of those that a mesh axis runs over, the one named last changes fastest.
Arguments:
- hidden_in: bfloat16 [32768, 4096], P(('ctx', 'tp')), may hold values from -6 to 6
- norm_gain: float32 [4096], replicated, may hold values from 0.5 to 1.5
- proj_weight: bfloat16 [4096, 8192], P(None, 'tp'), may hold values from -0.0625 to 0.0625
- conv_in: bfloat16 [32768, 8192], P('ctx', 'tp'), may hold values from -6 to 6
- conv_weight: float32 [4, 8192], P(None, 'tp'), may hold values from -3 to 3
- conv_bias: float32 [8192], P('tp'), may hold values from -3 to 3
- act_grad: bfloat16 [32768, 8192], P('ctx', 'tp'), may hold values from -6 to 6
Outputs:
- hidden_input_gradient: bfloat16 [32768, 4096], P(('ctx', 'tp'))
- norm_gain_gradient: float32 [4096], replicated
- taps_grad: float32 [4, 8192], P(None, 'tp')
- bias_grad: float32 [8192], P('tp')
All inputs are finite; a program needn't handle non-finite values.
Results may differ from a plain program's by a relative error of at most 0.013.
Values may be sent and summed in bfloat16 or wider, within the bound.
A program may use at most 32 MiB of HBM per device.

v0:
```python
import jax
import jax.numpy as jnp
from jax import lax
from jax.sharding import Mesh
from jax.sharding import PartitionSpec as P

CTX = ("ctx_0", "ctx_1", "ctx_2")
CTX_TP = ("ctx_0", "ctx_1", "ctx_2", "tp")


def from_behind(block, axis, distance):
    devices = range(lax.axis_size(axis))
    route = [(i - distance, i) for i in devices if i - distance in devices]
    return lax.ppermute(block, axis, route)


def over_axes(shard, axes):
    for axis in axes:
        shard = lax.psum(shard, axis)
    return shard


def preact_of(padded, taps, offset, count_tok):
    tap_count = taps.shape[0]
    return offset[None, :] + sum(
        (
            taps[index][None, :] * padded[tap_count - 1 - index : tap_count - 1 - index + count_tok]
            for index in range(tap_count)
        )
    )


def grad_of(preact, cotangent):
    sigmoid_v = jax.nn.sigmoid(preact)
    return cotangent.astype(jnp.float32) * sigmoid_v * (1.0 + preact * (1.0 - sigmoid_v))


def on_device(hidden_in, norm_gain, proj_weight, conv_in, conv_weight, conv_bias, act_grad):
    count_tok = conv_in.shape[0]
    tap_count = conv_weight.shape[0]
    edge_rows = tap_count - 1
    earlier = from_behind(conv_in[count_tok - edge_rows :], CTX, 1)
    padded = jnp.concatenate([earlier, conv_in], 0).astype(jnp.float32)
    preact = preact_of(padded, conv_weight, conv_bias, count_tok)
    pre_grad = grad_of(preact, act_grad)
    next_grad = from_behind(pre_grad[:edge_rows], CTX, -1)
    taps_part = jnp.stack(
        [
            jnp.sum(pre_grad * padded[edge_rows - index : edge_rows - index + count_tok], 0)
            for index in range(tap_count)
        ],
        0,
    )
    bias_part = jnp.sum(pre_grad, 0)
    taps_grad, bias_grad = (over_axes(taps_part, CTX), over_axes(bias_part, CTX))
    after = jnp.concatenate([pre_grad, next_grad], 0)
    in_grad = sum(
        (
            conv_weight[index][None, :] * after[index : index + count_tok]
            for index in range(tap_count)
        )
    ).astype(jnp.bfloat16)
    whole_term = lax.dot_general(
        in_grad, proj_weight, (((1,), (1,)), ((), ())), preferred_element_type=jnp.float32
    )
    normalized_gradient = lax.psum_scatter(
        whole_term.astype(jnp.bfloat16), "tp", scatter_dimension=0, tiled=True
    ).astype(jnp.float32)
    hidden_state = hidden_in.astype(jnp.float32)
    root_mean_square = jnp.sqrt(jnp.mean(hidden_state * hidden_state, -1, keepdims=True) + 1e-05)
    normalized_input = hidden_state / root_mean_square
    norm_gain_gradient = lax.psum(jnp.sum(normalized_gradient * normalized_input, 0), CTX_TP)
    scaled_gradient = norm_gain[None, :] * normalized_gradient
    mean_correction = jnp.mean(scaled_gradient * normalized_input, -1, keepdims=True)
    hidden_input_gradient = (
        (scaled_gradient - normalized_input * mean_correction) / root_mean_square
    ).astype(jnp.bfloat16)
    return (hidden_input_gradient, norm_gain_gradient, taps_grad, bias_grad)


def solution(mesh):
    finer = Mesh(
        mesh.devices.reshape(16, 4, 2, mesh.shape["tp"]), ("ctx_0", "ctx_1", "ctx_2", "tp")
    )
    return jax.shard_map(
        on_device,
        mesh=finer,
        in_specs=(
            P(CTX_TP, None),
            P(),
            P(None, "tp"),
            P(CTX, "tp"),
            P(None, "tp"),
            P("tp"),
            P(CTX, "tp"),
        ),
        out_specs=(P(CTX_TP, None), P(), P(None, "tp"), P("tp")),
        check_vma=False,
    )
```

profile of v0, /device:TPU:1, one launch (start us, length us, event | category | flops | bytes accessed | tf_op | source)
XLA Modules:
  0.0 477.1 jit_solution(408421029521848049)
XLA Ops:
  7.2 0.0 copy-start.3
  7.2 0.0 copy-start.1
  7.2 0.0 reduce-scatter.2.cloned.1.call-start
  7.2 0.8 slice.48
  8.0 4.5 collective-permute-start
  12.5 0.9 fusion.22
  13.4 10.7 %collective-permute-done = bf16[3,1024]{1,0:T(4,128)(2,1)S(1)} collective-permute-done((bf16[3,1024]{1,0:T(4,128)(2,1)S(1)}, bf16[3,1024]{1,0:T(4,128)(2,1)S(1)}, u32[]{:S(2)}, u32[]{:S(2)}) %collective-permute-start) | collective-permute-done | bytes 6176 | tf_op jit(solution)/shard_map/ppermute | solution.py:14
  24.1 1.2 maximum_convert_fusion
  25.2 0.0 copy-done.3
  25.3 0.0 copy-done.1
  25.3 1.3 multiply_reduce_fusion.3
  26.5 2.2 collective-permute-start.1
  28.7 2.9 collective-permute-done.1
  31.6 7.4 %convolution_convert_fusion = bf16[256,4096]{1,0:T(8,128)(2,1)} fusion(bf16[4096,1024]{1,0:T(8,128)(2,1)} %param.9, f32[3,1024]{1,0:T(4,128)S(1)} %collective-permute-done.1, f32[256,1024]{1,0:T(8,128)S(1)} %get-tuple-element.17, f32[1024]{0:T(1024)S(1)} %bitcast.18, f32[1024]{0:T(1024)S(1)} %bitcast.20, f32[1024]{0:T(1024)S(1)} %bitcast.16, f32[1024]{0:T(1024)S(1)} %bitcast.14), kind=kOutput, calls=%fused_computation | convolution fusion | flops 2151415808 | bytes 11563008 | tf_op jit(solution)/shard_map/dot_general | solution.py:63
  38.9 0.0 copy-start
  39.0 0.0 copy-start.2
  39.0 0.0 reduce-scatter.2.cloned.1.call-update
  39.0 0.9 copy-done
  39.9 0.2 fusion.15
  40.1 222.5 %all-reduce = (f32[4,1024]{1,0:T(4,128)S(1)}, f32[1024]{0:T(1024)S(1)}) all-reduce(f32[4,1024]{1,0:T(4,128)S(1)} %pad_maximum_fusion.1, f32[1024]{0:T(1024)S(1)} %get-tuple-element.8), channel_id=1, replica_groups=mesh['ctx_0'=16,'ctx_1'=4,'ctx_2'=2,'tp'=8] {'ctx_0'}, use_global_device_ids=true, to_apply=%region_9.0 | all-reduce | flops 5120 | bytes 40960 | tf_op jit(solution)/shard_map/psum | solution.py:19
  262.6 10.9 %all-reduce.1 = (f32[4,1024]{1,0:T(4,128)S(1)}, f32[1024]{0:T(1024)S(1)}) all-reduce(f32[4,1024]{1,0:T(4,128)S(1)} %get-tuple-element.11, f32[1024]{0:T(1024)S(1)} %get-tuple-element.12), channel_id=1, replica_groups=mesh['ctx_0'=16,'ctx_1'=4,'ctx_2'=2,'tp'=8] {'ctx_1'}, use_global_device_ids=true, to_apply=%region_10.0 | all-reduce | flops 5120 | bytes 40960 | tf_op jit(solution)/shard_map/psum | solution.py:19
  273.6 10.4 %all-reduce.2 = (f32[4,1024]{1,0:T(4,128)}, f32[1024]{0:T(1024)}) all-reduce(f32[4,1024]{1,0:T(4,128)S(1)} %get-tuple-element.13, f32[1024]{0:T(1024)S(1)} %get-tuple-element.14), channel_id=1, replica_groups=mesh['ctx_0'=16,'ctx_1'=4,'ctx_2'=2,'tp'=8] {'ctx_2'}, use_global_device_ids=true, to_apply=%region_11.0 | all-reduce | flops 5120 | bytes 40960 | tf_op jit(solution)/shard_map/psum | solution.py:19
  284.0 29.8 %reduce-scatter.2.cloned.1.call-done = bf16[32,4096]{1,0:T(8,128)(2,1)} async-done(((bf16[256,4096]{1,0:T(8,128)(2,1)}), bf16[32,4096]{1,0:T(8,128)(2,1)}) %reduce-scatter.2.cloned.1.call-update) | async-done | bytes 262160 | tf_op jit(solution)/shard_map/reduce_scatter | solution.py:66
  313.8 0.0 copy-done.2
  313.8 1.3 fusion.14
  315.1 153.4 %psum.49 = f32[4096]{0:T(1024)} all-reduce(f32[4096]{0:T(1024)S(1)} %get-tuple-element.9), channel_id=1, replica_groups=mesh['ctx_0'=16,'ctx_1'=4,'ctx_2'=2,'tp'=8] {'ctx_0','ctx_1','ctx_2','tp'}, use_global_device_ids=true, to_apply=%region_4.0 | all-reduce | flops 4096 | bytes 32768 | tf_op jit(solution)/shard_map/psum | solution.py:72
  468.5 1.8 fusion.13
  (4 shorter events, 0.0 us)
Async XLA Ops:
  7.2 18.1 %copy-start.3 = (f32[1024]{0:T(1024)S(1)}, f32[1024]{0:T(1024)}, u32[]{:S(2)}) copy-start(f32[1024]{0:T(1024)} %param.12) | copy-start | bytes 12292
  7.2 18.1 %copy-start.1 = (bf16[256,1024]{1,0:T(8,128)(2,1)S(1)}, bf16[256,1024]{1,0:T(8,128)(2,1)}, u32[]{:S(2)}) copy-start(bf16[256,1024]{1,0:T(8,128)(2,1)} %param.13) | copy-start | bytes 1572868
  7.2 306.6 %reduce-scatter.2.cloned.1.call-start = ((), (), s32[]{:S(2)}) async-start(), calls=%async_computation.1 | async-start | bytes 2359296 | tf_op jit(solution)/shard_map/reduce_scatter | solution.py:66
  8.0 16.0 %collective-permute-start = (bf16[3,1024]{1,0:T(4,128)(2,1)S(1)}, bf16[3,1024]{1,0:T(4,128)(2,1)S(1)}, u32[]{:S(2)}, u32[]{:S(2)}) collective-permute-start(bf16[3,1024]{1,0:T(4,128)(2,1)S(1)} %slice.48), channel_id=1, source_target_pairs={{0,8},{8,16},{16,24},{24,32},{32,40},{40,48},{48,56},{56,64},{64,7... | collective-permute-start | bytes 18440 | tf_op jit(solution)/shard_map/ppermute | solution.py:14
  26.5 5.1 %collective-permute-start.1 = (f32[3,1024]{1,0:T(4,128)S(1)}, f32[3,1024]{1,0:T(4,128)S(1)}, u32[]{:S(2)}, u32[]{:S(2)}) collective-permute-start(f32[3,1024]{1,0:T(4,128)S(1)} %slice.64), channel_id=1, source_target_pairs={{8,0},{16,8},{24,16},{32,24},{40,32},{48,40},{56,48},{64,56},{72,6... | collective-permute-start | bytes 36872 | tf_op jit(solution)/shard_map/ppermute | solution.py:14
  38.9 0.9 copy-start
  39.0 274.8 %copy-start.2 = (f32[4096]{0:T(1024)S(1)}, f32[4096]{0:T(1024)}, u32[]{:S(2)}) copy-start(f32[4096]{0:T(1024)} %param.8) | copy-start | bytes 49156
Sparse Core Ops, SparseCore 0:
  39.1 274.6 reduce-scatter.1
where the time goes:
time: 478 us; the launch traced here: 477 us
  blocking collectives  397 us (83%)
  waiting for transfers between devices  43.4 us (9%)
  between operations  14.1 us (3%)
  matrix products  7.35 us (2%)
  starting transfers between devices  6.69 us (1%)
  other arithmetic  5.76 us (1%)
    psum x3, blocking collectives, over_axes(): shard = lax.psum(shard, axis)  244 us
    psum x1, blocking collectives, on_device(): lax.psum(jnp.sum(normalized_gradient * normalized_input, 0), CTX_TP)  153 us
    reduce_scatter x1, waiting for transfers between devices, on_device(): lax.psum_scatter(whole_term.astype(jnp.bfloat16), 'tp', scatter_dimension...  29.8 us
    ppermute x2, waiting for transfers between devices, from_behind(): return lax.ppermute(block, axis, route)  13.5 us
  transfers between devices with their start and end apart: 3, of which 3 were waited for; matrix products, arithmetic and copies ran while one was open for 0% of the time, Pallas kernels for 0%

commit v1 on v0

v1 whole, which is shorter than its diff:
```python
import jax
import jax.numpy as jnp
from jax import lax
from jax.experimental import pallas as pl
from jax.experimental.pallas import tpu as pltpu
from jax.sharding import Mesh
from jax.sharding import PartitionSpec as P

MESH = pl.DeviceIdType.MESH
NZL, NX, NC, NY, NZH = 16, 4, 2, 4, 2
NZ = NZL * NZH
NPLANE = NX * NC * NY
NLINE = NX * NC
NCTX = NZL * NX * NC
ROWS = 256
CHAN = 1024
DIM = 4096
NCH = 8
WIDE = DIM // NCH
PER = WIDE // 128
OWN = 32
PAIR = 64
TILE = 16
NEAR = 4
F32 = jnp.float32
BF16 = jnp.bfloat16


def rem(a, b):
    return lax.rem(a, b)


def z_device(z):
    z = rem(z, NZ)
    return {"zh": z // NZL, "zl": rem(z, NZL)}


def plane_device(q):
    return {"x": q // (NY * NC), "y": rem(q // NC, NY), "c": rem(q, NC)}


def line_device(q):
    return {"x": q // NC, "c": rem(q, NC)}


def ctx_device(n):
    return {"zl": n // NLINE, "x": rem(n // NC, NX), "c": rem(n, NC)}


def kernel(
    hid_h, gain_h, w_h, conv_h, cw_h, cb_h, act_h,
    out_h, gain_o, taps_o, bias_o,
    hid, gain, w, conv, cw, cb, act, out,
    hprev, hconv, hact,
    xf, pg, ing, tacc,
    pbuf, ybuf, own, zs, zr, inv,
    gbuf, gr, za, ga, tpc, tr, tz, tf,
    in_sem, w_sem, out_sem, hs_sem, hr_sem, ys_sem, yr_sem, zs_sem, zr_sem, small_s, small_r, far,
):
    zl = lax.axis_index("zl")
    zh = lax.axis_index("zh")
    x = lax.axis_index("x")
    y = lax.axis_index("y")
    c = lax.axis_index("c")
    z = zh * NZL + zl
    q = (x * NY + y) * NC + c
    line = x * NC + c
    n = zl * NLINE + line
    has_next = n < NCTX - 1
    has_prev = n > 0
    far_next = jnp.logical_and(line == NLINE - 1, has_next)
    far_prev = jnp.logical_and(line == 0, has_prev)

    def remote(src, dst, send, recv, device):
        return pltpu.make_async_remote_copy(
            src_ref=src, dst_ref=dst, send_sem=send, recv_sem=recv, device_id=device, device_id_type=MESH
        )

    def drain(ref, sem):
        pltpu.make_async_copy(ref, ref, sem).wait()

    loads = [
        pltpu.make_async_copy(a, b, in_sem.at[i])
        for i, (a, b) in enumerate(
            [(conv_h, conv), (act_h, act), (cw_h, cw), (cb_h, cb), (hid_h, hid), (gain_h, gain)]
        )
    ]
    for load in loads:
        load.start()

    def w_load(j):
        rows = pl.ds(pl.multiple_of(j * WIDE, WIDE), WIDE)
        return pltpu.make_async_copy(w_h.at[rows], w.at[rows], w_sem.at[j])

    @pl.loop(0, NCH)
    def _(j):
        w_load(j).start()

    barrier = pltpu.get_barrier_semaphore()

    @pl.when(has_next)
    def _():
        @pl.when(far_next)
        def _():
            pl.semaphore_signal(barrier, 1, device_id=ctx_device(n + 1), device_id_type=MESH)

    @pl.when(far_prev)
    def _():
        pl.semaphore_signal(barrier, 1, device_id=ctx_device(n - 1), device_id_type=MESH)

    @pl.loop(1, NPLANE)
    def _(k):
        pl.semaphore_signal(barrier, 1, device_id=plane_device(rem(q + k, NPLANE)), device_id_type=MESH)

    @pl.loop(1, NEAR + 1)
    def _(k):
        pl.semaphore_signal(barrier, 1, device_id=z_device(z + k), device_id_type=MESH)
        pl.semaphore_signal(barrier, 1, device_id=z_device(z + NZ - k), device_id_type=MESH)

    xf[0:8, :] = jnp.zeros((8, CHAN), F32)
    tacc[...] = jnp.zeros_like(tacc)
    loads[0].wait()

    @pl.loop(0, ROWS // TILE)
    def _(i):
        t = pl.multiple_of(i * TILE, TILE)
        xf[pl.ds(t + 8, TILE), :] = conv[pl.ds(t, TILE), :].astype(F32)

    for load in loads[1:4]:
        load.wait()

    def grad_tile(t, rows, cotangent):
        above = xf[pl.ds(t, rows + 8), :]
        xs = [above[8 - k : 8 - k + rows] for k in range(4)]
        pre = cb[0:1, :] + sum(cw[k : k + 1, :] * xs[k] for k in range(4))
        s = 1.0 / (1.0 + jnp.exp(-pre))
        return cotangent * s * (1.0 + pre * (1.0 - s)), xs

    def pass_one(i):
        t = pl.multiple_of(i * TILE, TILE)
        g, xs = grad_tile(t, TILE, act[pl.ds(t, TILE), :].astype(F32))
        pg[pl.ds(t, TILE), :] = g
        for k in range(5):
            term = g * xs[k] if k < 4 else g
            tacc[k] += term[0:8] + term[8:16]

    def pass_two(i):
        t = pl.multiple_of(i * TILE, TILE)
        below = pg[pl.ds(t, TILE + 8), :]
        total = sum(cw[k : k + 1, :] * below[k : k + TILE] for k in range(4))
        ing[pl.ds(t, TILE), :] = total.astype(BF16)

    last = ROWS // TILE - 1

    @pl.loop(1, last // 2)
    def _(i):
        pass_one(i)

    pl.semaphore_wait(
        barrier,
        NPLANE - 1 + 2 * NEAR + jnp.where(far_next, 1, 0) + jnp.where(far_prev, 1, 0),
    )
    to_next = remote(conv.at[pl.ds(ROWS - 16, 16)], hprev, hs_sem.at[0], hr_sem.at[0], ctx_device(jnp.minimum(n + 1, NCTX - 1)))
    to_prev = [
        remote(conv.at[pl.ds(0, 16)], hconv, hs_sem.at[1], hr_sem.at[1], ctx_device(jnp.maximum(n - 1, 0))),
        remote(act.at[pl.ds(0, 16)], hact, hs_sem.at[2], hr_sem.at[2], ctx_device(jnp.maximum(n - 1, 0))),
    ]

    @pl.when(has_next)
    def _():
        to_next.start()

    @pl.when(has_prev)
    def _():
        for copy in to_prev:
            copy.start()

    for step in (NEAR, NZ - NEAR):
        pl.semaphore_signal(far.at[0], 1, device_id=z_device(z + step), device_id_type=MESH)

    @pl.loop(last // 2, last + 1)
    def _(i):
        pass_one(i)

    @pl.loop(1, last)
    def _(i):
        pass_two(i)

    pl.semaphore_wait(far.at[0], 2)
    for step in (2 * NEAR, NZ - 2 * NEAR):
        pl.semaphore_signal(far.at[1], 1, device_id=z_device(z + step), device_id_type=MESH)

    @pl.when(has_prev)
    def _():
        to_next.wait_recv()
        xf[0:8, :] = hprev[8:16, :].astype(F32)

    pass_one(0)
    pass_two(0)

    @pl.when(has_next)
    def _():
        for copy in to_prev:
            copy.wait_recv()
        xf[ROWS + 8 : ROWS + 16, :] = hconv[0:8, :].astype(F32)
        g, _ = grad_tile(ROWS, 8, hact[0:8, :].astype(F32))
        pg[ROWS : ROWS + 8, :] = g

    @pl.when(jnp.logical_not(has_next))
    def _():
        pg[ROWS : ROWS + 8, :] = jnp.zeros((8, CHAN), F32)

    pass_two(last)

    def product(j):
        rows = pl.ds(pl.multiple_of(j * WIDE, WIDE), WIDE)
        w_load(j).wait()
        part = lax.dot_general(ing[...], w[rows, :], (((1,), (1,)), ((), ())), preferred_element_type=F32)
        pbuf[j] = part.astype(BF16)

    def y_copy(j, k):
        to = rem(y + k, NY)
        return remote(
            pbuf.at[j, pl.ds(pl.multiple_of(to * PAIR, PAIR), PAIR)],
            ybuf.at[j, y],
            ys_sem.at[j],
            yr_sem.at[j],
            {"y": to},
        )

    def y_send(j):
        for k in range(1, NY):
            y_copy(j, k).start()

    product(0)

    @pl.loop(1, NCH)
    def _(j):
        product(j)
        y_send(j - 1)

    y_send(NCH - 1)

    sums = [jnp.sum(tacc[k], 0, keepdims=True) for k in range(5)]
    for p in range(NLINE):
        for k in range(5):
            tpc[p, k : k + 1, :] = sums[k][:, p * 128 : (p + 1) * 128]
        tpc[p, 5:8, :] = jnp.zeros((3, 128), F32)
    tr[line] = tpc[line]

    loads[4].wait()
    loads[5].wait()

    def squares(j, total):
        cols = pl.ds(pl.multiple_of(j * WIDE, WIDE), WIDE)
        h = hid[:, cols].astype(F32)
        h = h * h
        return total + sum(h[:, i * 128 : (i + 1) * 128] for i in range(PER))

    square = lax.fori_loop(0, NCH, squares, jnp.zeros((OWN, 128), F32))
    rms = jnp.sqrt(jnp.sum(square, -1, keepdims=True) * (1.0 / DIM) + 1e-05)
    inv[...] = jnp.broadcast_to(1.0 / rms, (OWN, 128))

    def line_copy(k, src, dst, i):
        return remote(src, dst, small_s.at[i], small_r.at[i], line_device(rem(line + k, NLINE)))

    @pl.loop(1, NLINE)
    def _(k):
        line_copy(k, tpc.at[rem(line + k, NLINE)], tr.at[line], 0).start()

    pl.semaphore_wait(far.at[1], 2)

    def z_copy(j):
        return remote(zs.at[j], zr.at[j], zs_sem.at[j], zr_sem.at[j], {"zh": 1 - zh})

    mine = pl.multiple_of(zh * OWN, OWN)
    other = pl.multiple_of((1 - zh) * OWN, OWN)

    @pl.loop(0, NCH)
    def _(j):
        drain(ybuf.at[j, pl.ds(0, NY - 1)], yr_sem.at[j])
        ybuf[j, y] = pbuf[j, pl.ds(pl.multiple_of(y * PAIR, PAIR), PAIR), :]

        def total(start):
            return sum(ybuf[j, s, pl.ds(start, OWN), :].astype(F32) for s in range(NY))

        zs[j] = total(other).astype(BF16)
        own[j] = total(mine)
        z_copy(j).start()

    drain(tr.at[pl.ds(0, NLINE - 1)], small_r.at[0])
    tz[zl] = jnp.sum(tr[...], 0)

    def zl_copy(k):
        to = rem(zl + k, NZL)
        return remote(tz.at[zl], tz.at[zl], small_s.at[1], small_r.at[1], {"zl": to})

    @pl.loop(1, NZL)
    def _(k):
        zl_copy(k).start()

    def xhat_of(j):
        cols = pl.ds(pl.multiple_of(j * WIDE, WIDE), WIDE)
        return hid[:, cols].astype(F32) * inv[:, 0:1]

    def gain_of(j):
        return gain[0:1, pl.ds(pl.multiple_of(j * WIDE, WIDE), WIDE)]

    def arrive(j, mean):
        z_copy(j).wait_recv()
        normed = own[j] + zr[j].astype(F32)
        own[j] = normed
        both = normed * xhat_of(j)
        sums = jnp.sum(both, 0, keepdims=True)
        for i in range(PER):
            gbuf[j * PER + i, 0:1, :] = sums[:, i * 128 : (i + 1) * 128]
        both = both * gain_of(j)
        mean = mean + sum(both[:, i * 128 : (i + 1) * 128] for i in range(PER))

        @pl.loop(0, PER)
        def _(i):
            p = j * PER + i

            @pl.when(p != q)
            def _():
                remote(
                    gbuf.at[p, pl.ds(0, 1)], gr.at[q, pl.ds(0, 1)], small_s.at[2], small_r.at[2], plane_device(p)
                ).start()

            @pl.when(p == q)
            def _():
                gr[q, 0:1, :] = gbuf[p, 0:1, :]

        return mean

    mean = lax.fori_loop(0, NCH, arrive, jnp.zeros((OWN, 128), F32))
    mean = jnp.sum(mean, -1, keepdims=True) * (1.0 / DIM)

    drain(tz.at[pl.ds(0, NZL - 1)], small_r.at[1])
    tf[line] = jnp.sum(tz[...], 0)

    drain(gr.at[pl.ds(0, NPLANE - 1), pl.ds(0, 1)], small_r.at[2])
    za[z, 0:1, :] = jnp.sum(gr[:, 0:1, :], 0)

    @pl.loop(1, NLINE)
    def _(k):
        line_copy(k, tf.at[line], tf.at[line], 3).start()

    @pl.loop(1, NZ)
    def _(k):
        remote(
            za.at[z, pl.ds(0, 1)], za.at[z, pl.ds(0, 1)], small_s.at[4], small_r.at[4], z_device(z + k)
        ).start()

    @pl.loop(0, NCH)
    def _(j):
        cols = pl.ds(pl.multiple_of(j * WIDE, WIDE), WIDE)
        value = (gain_of(j) * own[j] - xhat_of(j) * mean) * inv[:, 0:1]
        out[:, cols] = value.astype(BF16)

    store = pltpu.make_async_copy(out, out_h, out_sem)
    store.start()

    drain(tf.at[pl.ds(0, NLINE - 1)], small_r.at[3])
    for p in range(NLINE):
        taps_o[:, p * 128 : (p + 1) * 128] = tf[p, 0:4, :]
        bias_o[:, p * 128 : (p + 1) * 128] = tf[p, 4:5, :]

    drain(za.at[pl.ds(0, NZ - 1), pl.ds(0, 1)], small_r.at[4])
    ga[q, 0:1, :] = jnp.sum(za[:, 0:1, :], 0)

    @pl.loop(1, NPLANE)
    def _(k):
        remote(
            ga.at[q, pl.ds(0, 1)], ga.at[q, pl.ds(0, 1)], small_s.at[5], small_r.at[5], plane_device(rem(q + k, NPLANE))
        ).start()

    @pl.when(has_next)
    def _():
        to_next.wait_send()

    @pl.when(has_prev)
    def _():
        for copy in to_prev:
            copy.wait_send()

    @pl.loop(0, NCH)
    def _(j):
        drain(ybuf.at[j, pl.ds(0, NY - 1)], ys_sem.at[j])
        z_copy(j).wait_send()

    drain(tr.at[pl.ds(0, NLINE - 1)], small_s.at[0])
    drain(tz.at[pl.ds(0, NZL - 1)], small_s.at[1])
    drain(gr.at[pl.ds(0, NPLANE - 1), pl.ds(0, 1)], small_s.at[2])
    drain(tf.at[pl.ds(0, NLINE - 1)], small_s.at[3])
    drain(za.at[pl.ds(0, NZ - 1), pl.ds(0, 1)], small_s.at[4])
    store.wait()
    drain(ga.at[pl.ds(0, NPLANE - 1), pl.ds(0, 1)], small_r.at[5])
    gain_o[...] = ga[:, 0, :]
    drain(ga.at[pl.ds(0, NPLANE - 1), pl.ds(0, 1)], small_s.at[5])


def on_device(hidden_in, norm_gain, proj_weight, conv_in, conv_weight, conv_bias, act_grad):
    vmem = pltpu.VMEM
    dma = pltpu.SemaphoreType.DMA
    out, gain, taps, bias = pl.pallas_call(
        kernel,
        out_shape=(
            jax.ShapeDtypeStruct((OWN, DIM), BF16),
            jax.ShapeDtypeStruct((NPLANE, 128), F32),
            jax.ShapeDtypeStruct((4, CHAN), F32),
            jax.ShapeDtypeStruct((1, CHAN), F32),
        ),
        in_specs=[pl.BlockSpec(memory_space=pl.ANY)] * 7,
        out_specs=(pl.BlockSpec(memory_space=pl.ANY),) + (pl.BlockSpec(memory_space=vmem),) * 3,
        scratch_shapes=[
            vmem((OWN, DIM), BF16),
            vmem((1, DIM), F32),
            vmem((DIM, CHAN), BF16),
            vmem((ROWS, CHAN), BF16),
            vmem((4, CHAN), F32),
            vmem((1, CHAN), F32),
            vmem((ROWS, CHAN), BF16),
            vmem((OWN, DIM), BF16),
            vmem((16, CHAN), BF16),
            vmem((16, CHAN), BF16),
            vmem((16, CHAN), BF16),
            vmem((ROWS + 16, CHAN), F32),
            vmem((ROWS + 8, CHAN), F32),
            vmem((ROWS, CHAN), BF16),
            vmem((5, 8, CHAN), F32),
            vmem((NCH, ROWS, WIDE), BF16),
            vmem((NCH, NY, PAIR, WIDE), BF16),
            vmem((NCH, OWN, WIDE), F32),
            vmem((NCH, OWN, WIDE), BF16),
            vmem((NCH, OWN, WIDE), BF16),
            vmem((OWN, 128), F32),
            vmem((NPLANE, 8, 128), F32),
            vmem((NPLANE, 8, 128), F32),
            vmem((NZ, 8, 128), F32),
            vmem((NPLANE, 8, 128), F32),
            vmem((NLINE, 8, 128), F32),
            vmem((NLINE, 8, 128), F32),
            vmem((NZL, 8, 128), F32),
            vmem((NLINE, 8, 128), F32),
            dma((6,)),
            dma((NCH,)),
            dma,
            dma((3,)),
            dma((3,)),
            dma((NCH,)),
            dma((NCH,)),
            dma((NCH,)),
            dma((NCH,)),
            dma((6,)),
            dma((6,)),
            pltpu.SemaphoreType.REGULAR((2,)),
        ],
        compiler_params=pltpu.CompilerParams(collective_id=0, has_side_effects=True),
        name="layer_backward",
    )(
        hidden_in,
        norm_gain.reshape(1, DIM),
        proj_weight,
        conv_in,
        conv_weight,
        conv_bias.reshape(1, CHAN),
        act_grad,
    )
    return out, gain.reshape(DIM), taps, bias.reshape(CHAN)


def solution(mesh):
    finer = Mesh(mesh.devices.reshape(NZL, NX, NC, NY, NZH), ("zl", "x", "c", "y", "zh"))
    ctx = ("zl", "x", "c")
    tp = ("y", "zh")
    return jax.shard_map(
        on_device,
        mesh=finer,
        in_specs=(
            P(ctx + tp, None),
            P(),
            P(None, tp),
            P(ctx, tp),
            P(None, tp),
            P(tp),
            P(ctx, tp),
        ),
        out_specs=(P(ctx + tp, None), P(), P(None, tp), P(tp)),
        check_vma=False,
    )
```

time: 478 us -> 121 us (0.25)
  blocking collectives: 397 us -> 0 us
  Pallas kernels: 0 us -> 114 us
  waiting for transfers between devices: 43.4 us -> 0 us
  between operations: 14.1 us -> 0.64 us
  matrix products: 7.35 us -> 0 us
  starting transfers between devices: 6.69 us -> 0 us
  other arithmetic: 5.76 us -> 0 us
    psum x4 -> x0, blocking collectives: 397 us -> none  [the longest x3 244 us: over_axes(): shard = lax.psum(shard, axis)]
    pallas_call x0 -> x1, Pallas kernels: none -> 114 us  [on_device(): pl.pallas_call(kernel, out_shape=(jax.ShapeDtypeStruct((OWN, DIM), BF16),...]
    reduce_scatter x1 -> x0, waiting for transfers between devices: 29.8 us -> none  [on_device(): lax.psum_scatter(whole_term.astype(jnp.bfloat16), 'tp', scatter_dimension...]
    ppermute x2 -> x0, waiting for transfers between devices: 13.5 us -> none  [from_behind(): return lax.ppermute(block, axis, route)]
    dot_general x1 -> x0, matrix products: 7.35 us -> none  [on_device(): lax.dot_general(in_grad, proj_weight, (((1,), (1,)), ((), ())), preferred...]
    ppermute x2 -> x0, starting transfers between devices: 6.65 us -> none  [from_behind(): return lax.ppermute(block, axis, route)]
  transfers between devices with their start and end apart: 3 -> 0, of which waited for: 3 -> 0; matrix products, arithmetic and copies ran while one was open for 0% -> 0% of each run, Pallas kernels for 0% -> 0%
where the time goes in v1:
time: 121 us; the launch traced here: 120 us
  Pallas kernels  114 us (94%)
  local copies, waits for them, and re-layouts  5.59 us (5%)
    pallas_call x1, Pallas kernels, on_device(): pl.pallas_call(kernel, out_shape=(jax.ShapeDtypeStruct((OWN, DIM), BF16),...  114 us
    unnamed x4, local copies, waits for them, and re-layouts  5.59 us

profile of v1, /device:TPU:1, one launch (start us, length us, event | category | flops | bytes accessed | tf_op | source)
XLA Modules:
  0.0 120.2 jit_solution(1226735681607870012)
XLA Ops:
  0.6 114.0 %layer_backward.1 = (bf16[32,4096]{1,0:T(8,128)(2,1)}, f32[32,128]{1,0:T(8,128)}, f32[4,1024]{1,0:T(4,128)}, f32[1,1024]{1,0:T(1,128)}) custom-call(bf16[32,4096]{1,0:T(8,128)(2,1)} %hid_h.1, f32[1,4096]{1,0:T(1,128)} %bitcast.4, bf16[4096,1024]{1,0:T(8,128)(2,1)} %w_h.1, bf16[256,1024]{1,0:T(8,128)(2,1)} %conv_h.1, f32[4,1024]{1,0:T(4,128)} %cw_h.1, ...), custom_call_target="tpu_custom_call" | custom-call | tf_op jit(solution)/shard_map/layer_backward/pallas_call | solution.py:406
  114.6 1.7 %copy.15 = bf16[32,4096]{1,0:T(8,128)(2,1)} copy(bf16[32,4096]{1,0:T(8,128)(2,1)} %get-tuple-element.16) | data formatting | bytes 524288
  116.3 1.3 %copy.16 = f32[4096]{0:T(1024)} copy(f32[4096]{0:T(1024)} %bitcast.5) | data formatting | bytes 32768
  117.6 1.3 %copy.17 = f32[4,1024]{1,0:T(4,128)} copy(f32[4,1024]{1,0:T(4,128)} %get-tuple-element.18) | data formatting | bytes 32768
  118.9 1.3 %copy.18 = f32[1024]{0:T(1024)} copy(f32[1024]{0:T(1024)} %bitcast.7) | data formatting | bytes 8192

commit v2 on v1

--- a/solution.py
+++ b/solution.py
@@ -15,13 +15,16 @@
 ROWS = 256
 CHAN = 1024
 DIM = 4096
-NCH = 8
+NCH = 16
 WIDE = DIM // NCH
 PER = WIDE // 128
 OWN = 32
 PAIR = 64
 TILE = 16
 NEAR = 4
+WINDOW = 8
+FIRST = 10
+GROUP = 4
 F32 = jnp.float32
 BF16 = jnp.bfloat16
 
@@ -49,13 +52,13 @@
 
 def kernel(
     hid_h, gain_h, w_h, conv_h, cw_h, cb_h, act_h,
-    out_h, gain_o, taps_o, bias_o,
-    hid, gain, w, conv, cw, cb, act, out,
+    out_o, gain_o, taps_o, bias_o,
+    hid, gain, w, conv, cw, cb, act,
     hprev, hconv, hact,
     xf, pg, ing, tacc,
-    pbuf, ybuf, own, zs, zr, inv,
-    gbuf, gr, za, ga, tpc, tr, tz, tf,
-    in_sem, w_sem, out_sem, hs_sem, hr_sem, ys_sem, yr_sem, zs_sem, zr_sem, small_s, small_r, far,
+    pbuf, ybuf, own, zs, zr, inv, mean,
+    gbuf, gr, za, ga, tpc, tr, tn, tz, tf,
+    in_sem, w_sem, hs_sem, hr_sem, ys_sem, yr_sem, zs_sem, zr_sem, small_s, small_r, far,
 ):
     zl = lax.axis_index("zl")
     zh = lax.axis_index("zh")
@@ -85,7 +88,32 @@
             [(conv_h, conv), (act_h, act), (cw_h, cw), (cb_h, cb), (hid_h, hid), (gain_h, gain)]
         )
     ]
-    for load in loads:
+    for load in loads[:4]:
+        load.start()
+
+    barrier = pltpu.get_barrier_semaphore()
+
+    @pl.loop(0, NEAR)
+    def _(k):
+        pl.semaphore_signal(barrier, 1, device_id=z_device(z + (NEAR - k)), device_id_type=MESH)
+        pl.semaphore_signal(barrier, 1, device_id=z_device(z + NZ - (NEAR - k)), device_id_type=MESH)
+
+    @pl.loop(1, NPLANE)
+    def _(k):
+        pl.semaphore_signal(barrier, 1, device_id=plane_device(rem(q + k, NPLANE)), device_id_type=MESH)
+
+    @pl.when(has_next)
+    def _():
+        @pl.when(far_next)
+        def _():
+            pl.semaphore_signal(barrier, 1, device_id=ctx_device(n + 1), device_id_type=MESH)
+
+    @pl.when(far_prev)
+    def _():
+        pl.semaphore_signal(barrier, 1, device_id=ctx_device(n - 1), device_id_type=MESH)
+
+
+    for load in loads[4:]:
         load.start()
 
     def w_load(j):
@@ -95,27 +123,6 @@
     @pl.loop(0, NCH)
     def _(j):
         w_load(j).start()
-
-    barrier = pltpu.get_barrier_semaphore()
-
-    @pl.when(has_next)
-    def _():
-        @pl.when(far_next)
-        def _():
-            pl.semaphore_signal(barrier, 1, device_id=ctx_device(n + 1), device_id_type=MESH)
-
-    @pl.when(far_prev)
-    def _():
-        pl.semaphore_signal(barrier, 1, device_id=ctx_device(n - 1), device_id_type=MESH)
-
-    @pl.loop(1, NPLANE)
-    def _(k):
-        pl.semaphore_signal(barrier, 1, device_id=plane_device(rem(q + k, NPLANE)), device_id_type=MESH)
-
-    @pl.loop(1, NEAR + 1)
-    def _(k):
-        pl.semaphore_signal(barrier, 1, device_id=z_device(z + k), device_id_type=MESH)
-        pl.semaphore_signal(barrier, 1, device_id=z_device(z + NZ - k), device_id_type=MESH)
 
     xf[0:8, :] = jnp.zeros((8, CHAN), F32)
     tacc[...] = jnp.zeros_like(tacc)
@@ -152,14 +159,21 @@
 
     last = ROWS // TILE - 1
 
-    @pl.loop(1, last // 2)
+    @pl.loop(1, last + 1)
     def _(i):
         pass_one(i)
+
+    @pl.loop(1, last)
+    def _(i):
+        pass_two(i)
 
     pl.semaphore_wait(
         barrier,
         NPLANE - 1 + 2 * NEAR + jnp.where(far_next, 1, 0) + jnp.where(far_prev, 1, 0),
     )
+    for step in (NEAR, NZ - NEAR):
+        pl.semaphore_signal(far.at[0], 1, device_id=z_device(z + step), device_id_type=MESH)
+
     to_next = remote(conv.at[pl.ds(ROWS - 16, 16)], hprev, hs_sem.at[0], hr_sem.at[0], ctx_device(jnp.minimum(n + 1, NCTX - 1)))
     to_prev = [
         remote(conv.at[pl.ds(0, 16)], hconv, hs_sem.at[1], hr_sem.at[1], ctx_device(jnp.maximum(n - 1, 0))),
@@ -174,17 +188,6 @@
     def _():
         for copy in to_prev:
             copy.start()
-
-    for step in (NEAR, NZ - NEAR):
-        pl.semaphore_signal(far.at[0], 1, device_id=z_device(z + step), device_id_type=MESH)
-
-    @pl.loop(last // 2, last + 1)
-    def _(i):
-        pass_one(i)
-
-    @pl.loop(1, last)
-    def _(i):
-        pass_two(i)
 
     pl.semaphore_wait(far.at[0], 2)
     for step in (2 * NEAR, NZ - 2 * NEAR):
@@ -232,72 +235,26 @@
         for k in range(1, NY):
             y_copy(j, k).start()
 
-    product(0)
-
-    @pl.loop(1, NCH)
-    def _(j):
+    def produce(j):
         product(j)
         y_send(j - 1)
 
-    y_send(NCH - 1)
-
-    sums = [jnp.sum(tacc[k], 0, keepdims=True) for k in range(5)]
-    for p in range(NLINE):
-        for k in range(5):
-            tpc[p, k : k + 1, :] = sums[k][:, p * 128 : (p + 1) * 128]
-        tpc[p, 5:8, :] = jnp.zeros((3, 128), F32)
-    tr[line] = tpc[line]
-
-    loads[4].wait()
-    loads[5].wait()
-
-    def squares(j, total):
-        cols = pl.ds(pl.multiple_of(j * WIDE, WIDE), WIDE)
-        h = hid[:, cols].astype(F32)
-        h = h * h
-        return total + sum(h[:, i * 128 : (i + 1) * 128] for i in range(PER))
-
-    square = lax.fori_loop(0, NCH, squares, jnp.zeros((OWN, 128), F32))
-    rms = jnp.sqrt(jnp.sum(square, -1, keepdims=True) * (1.0 / DIM) + 1e-05)
-    inv[...] = jnp.broadcast_to(1.0 / rms, (OWN, 128))
-
-    def line_copy(k, src, dst, i):
-        return remote(src, dst, small_s.at[i], small_r.at[i], line_device(rem(line + k, NLINE)))
-
-    @pl.loop(1, NLINE)
-    def _(k):
-        line_copy(k, tpc.at[rem(line + k, NLINE)], tr.at[line], 0).start()
-
-    pl.semaphore_wait(far.at[1], 2)
+        @pl.when(j == NCH - 1)
+        def _():
+            y_send(j)
+
+    product(0)
+
+    @pl.loop(1, FIRST)
+    def _(j):
+        produce(j)
+
 
     def z_copy(j):
         return remote(zs.at[j], zr.at[j], zs_sem.at[j], zr_sem.at[j], {"zh": 1 - zh})
 
     mine = pl.multiple_of(zh * OWN, OWN)
     other = pl.multiple_of((1 - zh) * OWN, OWN)
-
-    @pl.loop(0, NCH)
-    def _(j):
-        drain(ybuf.at[j, pl.ds(0, NY - 1)], yr_sem.at[j])
-        ybuf[j, y] = pbuf[j, pl.ds(pl.multiple_of(y * PAIR, PAIR), PAIR), :]
-
-        def total(start):
-            return sum(ybuf[j, s, pl.ds(start, OWN), :].astype(F32) for s in range(NY))
-
-        zs[j] = total(other).astype(BF16)
-        own[j] = total(mine)
-        z_copy(j).start()
-
-    drain(tr.at[pl.ds(0, NLINE - 1)], small_r.at[0])
-    tz[zl] = jnp.sum(tr[...], 0)
-
-    def zl_copy(k):
-        to = rem(zl + k, NZL)
-        return remote(tz.at[zl], tz.at[zl], small_s.at[1], small_r.at[1], {"zl": to})
-
-    @pl.loop(1, NZL)
-    def _(k):
-        zl_copy(k).start()
 
     def xhat_of(j):
         cols = pl.ds(pl.multiple_of(j * WIDE, WIDE), WIDE)
@@ -306,7 +263,7 @@
     def gain_of(j):
         return gain[0:1, pl.ds(pl.multiple_of(j * WIDE, WIDE), WIDE)]
 
-    def arrive(j, mean):
+    def arrive(j):
         z_copy(j).wait_recv()
         normed = own[j] + zr[j].astype(F32)
         own[j] = normed
@@ -315,7 +272,7 @@
         for i in range(PER):
             gbuf[j * PER + i, 0:1, :] = sums[:, i * 128 : (i + 1) * 128]
         both = both * gain_of(j)
-        mean = mean + sum(both[:, i * 128 : (i + 1) * 128] for i in range(PER))
+        mean[...] += sum(both[:, i * 128 : (i + 1) * 128] for i in range(PER))
 
         @pl.loop(0, PER)
         def _(i):
@@ -331,40 +288,130 @@
             def _():
                 gr[q, 0:1, :] = gbuf[p, 0:1, :]
 
-        return mean
-
-    mean = lax.fori_loop(0, NCH, arrive, jnp.zeros((OWN, 128), F32))
-    mean = jnp.sum(mean, -1, keepdims=True) * (1.0 / DIM)
-
-    drain(tz.at[pl.ds(0, NZL - 1)], small_r.at[1])
-    tf[line] = jnp.sum(tz[...], 0)
+    def forward(j):
+        drain(ybuf.at[j, pl.ds(0, NY - 1)], yr_sem.at[j])
+        ybuf[j, y] = pbuf[j, pl.ds(pl.multiple_of(y * PAIR, PAIR), PAIR), :]
+
+        def total(start):
+            return sum(ybuf[j, s, pl.ds(start, OWN), :].astype(F32) for s in range(NY))
+
+        zs[j] = total(other).astype(BF16)
+        own[j] = total(mine)
+        z_copy(j).start()
+
+    mean[...] = jnp.zeros_like(mean)
+    pl.semaphore_wait(far.at[1], 2)
+
+    @pl.loop(0, WINDOW)
+    def _(j):
+        forward(j)
+
+        @pl.when(j + FIRST < NCH)
+        def _():
+            produce(j + FIRST)
+
+    @pl.loop(FIRST + WINDOW, NCH)
+    def _(j):
+        produce(j)
+
+    sums = [jnp.sum(tacc[k], 0, keepdims=True) for k in range(5)]
+    for p in range(NLINE):
+        for k in range(5):
+            tpc[p, k : k + 1, :] = sums[k][:, p * 128 : (p + 1) * 128]
+    tr[line, 0:5, :] = tpc[line, 0:5, :]
+
+    loads[4].wait()
+    loads[5].wait()
+
+    def squares(j, total):
+        cols = pl.ds(pl.multiple_of(j * WIDE, WIDE), WIDE)
+        h = hid[:, cols].astype(F32)
+        h = h * h
+        return total + sum(h[:, i * 128 : (i + 1) * 128] for i in range(PER))
+
+    square = lax.fori_loop(0, NCH, squares, jnp.zeros((OWN, 128), F32))
+    rms = jnp.sqrt(jnp.sum(square, -1, keepdims=True) * (1.0 / DIM) + 1e-05)
+    inv[...] = jnp.broadcast_to(1.0 / rms, (OWN, 128))
+
+    def line_copy(k, src, dst, i):
+        return remote(src, dst, small_s.at[i], small_r.at[i], line_device(rem(line + k, NLINE)))
+
+    @pl.loop(1, NLINE)
+    def _(k):
+        line_copy(k, tpc.at[rem(line + k, NLINE), pl.ds(0, 5)], tr.at[line, pl.ds(0, 5)], 0).start()
+
+    def near_sums():
+        drain(tr.at[pl.ds(0, NLINE - 1), pl.ds(0, 5)], small_r.at[0])
+        tn[rem(zl, GROUP), 0:5, :] = jnp.sum(tr[:, 0:5, :], 0)
+
+        def near_copy(k):
+            mine = tn.at[rem(zl, GROUP), pl.ds(0, 5)]
+            to = zl - rem(zl, GROUP) + rem(zl + k, GROUP)
+            return remote(mine, mine, small_s.at[1], small_r.at[1], {"zl": to})
+
+        @pl.loop(1, GROUP)
+        def _(k):
+            near_copy(k).start()
+
+    def far_sums():
+        drain(tn.at[pl.ds(0, GROUP - 1), pl.ds(0, 5)], small_r.at[1])
+        tz[zl // GROUP, 0:5, :] = jnp.sum(tn[:, 0:5, :], 0)
+
+        def far_copy(k):
+            mine = tz.at[zl // GROUP, pl.ds(0, 5)]
+            return remote(mine, mine, small_s.at[6], small_r.at[6], {"zl": rem(zl + k * GROUP, NZL)})
+
+        @pl.loop(1, NZL // GROUP)
+        def _(k):
+            far_copy(k).start()
+
+    @pl.loop(WINDOW, NCH)
+    def _(j):
+        forward(j)
+
+        arrive(j - WINDOW)
+
+        @pl.when(j == NCH - 4)
+        def _():
+            near_sums()
+
+        @pl.when(j == NCH - 1)
+        def _():
+            far_sums()
+
+    @pl.loop(NCH - WINDOW, NCH)
+    def _(j):
+        arrive(j)
 
     drain(gr.at[pl.ds(0, NPLANE - 1), pl.ds(0, 1)], small_r.at[2])
     za[z, 0:1, :] = jnp.sum(gr[:, 0:1, :], 0)
 
-    @pl.loop(1, NLINE)
-    def _(k):
-        line_copy(k, tf.at[line], tf.at[line], 3).start()
-
-    @pl.loop(1, NZ)
-    def _(k):
+    def z_share(k):
         remote(
             za.at[z, pl.ds(0, 1)], za.at[z, pl.ds(0, 1)], small_s.at[4], small_r.at[4], z_device(z + k)
         ).start()
 
+    z_share(NZ // 2)
+
+    @pl.loop(1, NZ // 2)
+    def _(k):
+        z_share(NZ // 2 - k)
+        z_share(NZ // 2 + k)
+
+    average = jnp.sum(mean[...], -1, keepdims=True) * (1.0 / DIM)
+
     @pl.loop(0, NCH)
     def _(j):
         cols = pl.ds(pl.multiple_of(j * WIDE, WIDE), WIDE)
-        value = (gain_of(j) * own[j] - xhat_of(j) * mean) * inv[:, 0:1]
-        out[:, cols] = value.astype(BF16)
-
-    store = pltpu.make_async_copy(out, out_h, out_sem)
-    store.start()
-
-    drain(tf.at[pl.ds(0, NLINE - 1)], small_r.at[3])
-    for p in range(NLINE):
-        taps_o[:, p * 128 : (p + 1) * 128] = tf[p, 0:4, :]
-        bias_o[:, p * 128 : (p + 1) * 128] = tf[p, 4:5, :]
+        value = (gain_of(j) * own[j] - xhat_of(j) * average) * inv[:, 0:1]
+        out_o[:, cols] = value.astype(BF16)
+
+    drain(tz.at[pl.ds(0, NZL // GROUP - 1), pl.ds(0, 5)], small_r.at[6])
+    tf[line, 0:5, :] = jnp.sum(tz[:, 0:5, :], 0)
+
+    @pl.loop(1, NLINE)
+    def _(k):
+        line_copy(k, tf.at[line, pl.ds(0, 5)], tf.at[line, pl.ds(0, 5)], 3).start()
 
     drain(za.at[pl.ds(0, NZ - 1), pl.ds(0, 1)], small_r.at[4])
     ga[q, 0:1, :] = jnp.sum(za[:, 0:1, :], 0)
@@ -375,6 +422,11 @@
             ga.at[q, pl.ds(0, 1)], ga.at[q, pl.ds(0, 1)], small_s.at[5], small_r.at[5], plane_device(rem(q + k, NPLANE))
         ).start()
 
+    drain(tf.at[pl.ds(0, NLINE - 1), pl.ds(0, 5)], small_r.at[3])
+    for p in range(NLINE):
+        taps_o[:, p * 128 : (p + 1) * 128] = tf[p, 0:4, :]
+        bias_o[:, p * 128 : (p + 1) * 128] = tf[p, 4:5, :]
+
     @pl.when(has_next)
     def _():
         to_next.wait_send()
@@ -389,15 +441,37 @@
         drain(ybuf.at[j, pl.ds(0, NY - 1)], ys_sem.at[j])
         z_copy(j).wait_send()
 
-    drain(tr.at[pl.ds(0, NLINE - 1)], small_s.at[0])
-    drain(tz.at[pl.ds(0, NZL - 1)], small_s.at[1])
+    drain(tr.at[pl.ds(0, NLINE - 1), pl.ds(0, 5)], small_s.at[0])
+    drain(tn.at[pl.ds(0, GROUP - 1), pl.ds(0, 5)], small_s.at[1])
+    drain(tz.at[pl.ds(0, NZL // GROUP - 1), pl.ds(0, 5)], small_s.at[6])
     drain(gr.at[pl.ds(0, NPLANE - 1), pl.ds(0, 1)], small_s.at[2])
-    drain(tf.at[pl.ds(0, NLINE - 1)], small_s.at[3])
+    drain(tf.at[pl.ds(0, NLINE - 1), pl.ds(0, 5)], small_s.at[3])
     drain(za.at[pl.ds(0, NZ - 1), pl.ds(0, 1)], small_s.at[4])
-    store.wait()
     drain(ga.at[pl.ds(0, NPLANE - 1), pl.ds(0, 1)], small_r.at[5])
     gain_o[...] = ga[:, 0, :]
     drain(ga.at[pl.ds(0, NPLANE - 1), pl.ds(0, 1)], small_s.at[5])
+
+
+def hand_on(*arrays):
+    count = len(arrays)
+
+    def body(*refs):
+        sem = refs[2 * count]
+        copies = [pltpu.make_async_copy(refs[i], refs[count + i], sem.at[i]) for i in range(count)]
+        for copy in copies:
+            copy.start()
+        for copy in copies:
+            copy.wait()
+
+    return pl.pallas_call(
+        body,
+        out_shape=tuple(jax.ShapeDtypeStruct(a.shape, a.dtype) for a in arrays),
+        in_specs=[pl.BlockSpec(memory_space=pltpu.VMEM)] * count,
+        out_specs=(pl.BlockSpec(memory_space=pltpu.HBM),) * count,
+        scratch_shapes=[pltpu.SemaphoreType.DMA((count,))],
+        compiler_params=pltpu.CompilerParams(vmem_limit_bytes=4 << 20),
+        name="hand_on",
+    )(*arrays)
 
 
 def on_device(hidden_in, norm_gain, proj_weight, conv_in, conv_weight, conv_bias, act_grad):
@@ -411,8 +485,8 @@
             jax.ShapeDtypeStruct((4, CHAN), F32),
             jax.ShapeDtypeStruct((1, CHAN), F32),
         ),
-        in_specs=[pl.BlockSpec(memory_space=pl.ANY)] * 7,
-        out_specs=(pl.BlockSpec(memory_space=pl.ANY),) + (pl.BlockSpec(memory_space=vmem),) * 3,
+        in_specs=[pl.BlockSpec(memory_space=pltpu.HBM)] * 7,
+        out_specs=(pl.BlockSpec(memory_space=vmem),) * 4,
         scratch_shapes=[
             vmem((OWN, DIM), BF16),
             vmem((1, DIM), F32),
@@ -421,7 +495,6 @@
             vmem((4, CHAN), F32),
             vmem((1, CHAN), F32),
             vmem((ROWS, CHAN), BF16),
-            vmem((OWN, DIM), BF16),
             vmem((16, CHAN), BF16),
             vmem((16, CHAN), BF16),
             vmem((16, CHAN), BF16),
@@ -435,38 +508,45 @@
             vmem((NCH, OWN, WIDE), BF16),
             vmem((NCH, OWN, WIDE), BF16),
             vmem((OWN, 128), F32),
+            vmem((OWN, 128), F32),
             vmem((NPLANE, 8, 128), F32),
             vmem((NPLANE, 8, 128), F32),
             vmem((NZ, 8, 128), F32),
             vmem((NPLANE, 8, 128), F32),
             vmem((NLINE, 8, 128), F32),
             vmem((NLINE, 8, 128), F32),
-            vmem((NZL, 8, 128), F32),
+            vmem((GROUP, 8, 128), F32),
+            vmem((NZL // GROUP, 8, 128), F32),
             vmem((NLINE, 8, 128), F32),
             dma((6,)),
             dma((NCH,)),
-            dma,
             dma((3,)),
             dma((3,)),
             dma((NCH,)),
             dma((NCH,)),
             dma((NCH,)),
             dma((NCH,)),
-            dma((6,)),
-            dma((6,)),
+            dma((7,)),
+            dma((7,)),
             pltpu.SemaphoreType.REGULAR((2,)),
         ],
-        compiler_params=pltpu.CompilerParams(collective_id=0, has_side_effects=True),
+        compiler_params=pltpu.CompilerParams(collective_id=0, has_side_effects=True, vmem_limit_bytes=40 << 20),
         name="layer_backward",
     )(
-        hidden_in,
-        norm_gain.reshape(1, DIM),
-        proj_weight,
-        conv_in,
-        conv_weight,
-        conv_bias.reshape(1, CHAN),
-        act_grad,
+        *(
+            pltpu.with_memory_space_constraint(a, pltpu.HBM)
+            for a in (
+                hidden_in,
+                norm_gain.reshape(1, DIM),
+                proj_weight,
+                conv_in,
+                conv_weight,
+                conv_bias.reshape(1, CHAN),
+                act_grad,
+            )
+        )
     )
+    out, gain, taps, bias = hand_on(out, gain, taps, bias)
     return out, gain.reshape(DIM), taps, bias.reshape(CHAN)
 
 

time: 121 us -> 109 us (0.901)
  Pallas kernels: 114 us -> 108 us
  local copies, waits for them, and re-layouts: 5.59 us -> 0 us
    pallas_call x1, Pallas kernels: 114 us -> 107 us  [on_device(): pl.pallas_call(kernel, out_shape=(jax.ShapeDtypeStruct((OWN, DIM), BF16),...]
    unnamed x4 -> x0, local copies, waits for them, and re-layouts: 5.59 us -> none
where the time goes in v2:
time: 109 us
  Pallas kernels  108 us (99%)
    pallas_call x1, Pallas kernels, on_device(): pl.pallas_call(kernel, out_shape=(jax.ShapeDtypeStruct((OWN, DIM), BF16),...  107 us

profile of v2, /device:TPU:1, one launch (start us, length us, event | category | flops | bytes accessed | tf_op | source)
XLA Modules:
  0.0 108.7 jit_solution(14428252243671305107)
XLA Ops:
  0.6 107.3 %layer_backward.1 = (bf16[32,4096]{1,0:T(8,128)(2,1)S(1)}, f32[32,128]{1,0:T(8,128)S(1)}, f32[4,1024]{1,0:T(4,128)S(1)}, f32[1,1024]{1,0:T(1,128)S(1)}) custom-call(bf16[32,4096]{1,0:T(8,128)(2,1)} %hid_h.1, f32[1,4096]{1,0:T(1,128)} %bitcast.4, bf16[4096,1024]{1,0:T(8,128)(2,1)} %w_h.1, bf16[256,1024]{1,0:T(8,128)(2,1)} %conv_h.1, f32[4,1024]{1,0:T(4,128)} %cw_h.1, ...), custom_call_target="tpu_custom_call" | custom-call | tf_op jit(solution)/shard_map/layer_backward/pallas_call | solution.py:480
  108.0 0.7 hand_on.1

commit v3 on v2

--- a/solution.py
+++ b/solution.py
@@ -22,10 +22,17 @@
 PAIR = 64
 TILE = 16
 NEAR = 4
+AROUND = NY - 1 + NX - 1 + NC - 1
 WINDOW = 8
 FIRST = 10
+WLOADS = 4
 GROUP = 4
 F32 = jnp.float32
+CHIPS = sorted(
+    ((i, j) for i in range(NX) for j in range(NY)), key=lambda p: -min(p[0], NX - p[0]) - min(p[1], NY - p[1])
+)
+CHIP_X = sum(p[0] << (2 * i) for i, p in enumerate(CHIPS))
+CHIP_Y = sum(p[1] << (2 * i) for i, p in enumerate(CHIPS))
 BF16 = jnp.bfloat16
 
 
@@ -40,6 +47,15 @@
 
 def plane_device(q):
     return {"x": q // (NY * NC), "y": rem(q // NC, NY), "c": rem(q, NC)}
+
+
+def packed(table, i):
+    signed = table - (1 << 32) if table >> 31 else table
+    return lax.shift_right_logical(jnp.int32(signed), 2 * i) & 3
+
+
+def chip_at(place, core):
+    return {"x": packed(CHIP_X, place), "y": packed(CHIP_Y, place), "c": core}
 
 
 def line_device(q):
@@ -68,11 +84,13 @@
     z = zh * NZL + zl
     q = (x * NY + y) * NC + c
     line = x * NC + c
+    place = sum(jnp.where(jnp.logical_and(x == a, y == b), i, 0) for i, (a, b) in enumerate(CHIPS))
+    owner = c == NC - 1
     n = zl * NLINE + line
     has_next = n < NCTX - 1
     has_prev = n > 0
-    far_next = jnp.logical_and(line == NLINE - 1, has_next)
-    far_prev = jnp.logical_and(line == 0, has_prev)
+    chip_next = jnp.logical_and(c == NC - 1, has_next)
+    chip_prev = jnp.logical_and(c == 0, has_prev)
 
     def remote(src, dst, send, recv, device):
         return pltpu.make_async_remote_copy(
@@ -85,7 +103,14 @@
     loads = [
         pltpu.make_async_copy(a, b, in_sem.at[i])
         for i, (a, b) in enumerate(
-            [(conv_h, conv), (act_h, act), (cw_h, cw), (cb_h, cb), (hid_h, hid), (gain_h, gain)]
+            [
+                (conv_h, conv),
+                (act_h, act),
+                (cw_h, cw),
+                (cb_h, cb),
+                (hid_h, hid),
+                (gain_h, gain),
+            ]
         )
     ]
     for load in loads[:4]:
@@ -93,36 +118,40 @@
 
     barrier = pltpu.get_barrier_semaphore()
 
+    def greet(device):
+        pl.semaphore_signal(barrier, 1, device_id=device, device_id_type=MESH)
+
+    def plane_neighbours(visit):
+        for k in (2, 1, 3):
+            visit({"y": rem(y + k, NY)})
+            visit({"x": rem(x + k, NX)})
+        visit({"c": 1 - c})
+
     @pl.loop(0, NEAR)
     def _(k):
-        pl.semaphore_signal(barrier, 1, device_id=z_device(z + (NEAR - k)), device_id_type=MESH)
-        pl.semaphore_signal(barrier, 1, device_id=z_device(z + NZ - (NEAR - k)), device_id_type=MESH)
-
-    @pl.loop(1, NPLANE)
-    def _(k):
-        pl.semaphore_signal(barrier, 1, device_id=plane_device(rem(q + k, NPLANE)), device_id_type=MESH)
-
-    @pl.when(has_next)
-    def _():
-        @pl.when(far_next)
-        def _():
-            pl.semaphore_signal(barrier, 1, device_id=ctx_device(n + 1), device_id_type=MESH)
-
-    @pl.when(far_prev)
-    def _():
-        pl.semaphore_signal(barrier, 1, device_id=ctx_device(n - 1), device_id_type=MESH)
-
+        greet(z_device(z + (NEAR - k)))
+        greet(z_device(z + NZ - (NEAR - k)))
+
+    plane_neighbours(greet)
+
+    @pl.when(chip_next)
+    def _():
+        greet(ctx_device(n + 1))
+
+    @pl.when(chip_prev)
+    def _():
+        greet(ctx_device(n - 1))
 
     for load in loads[4:]:
         load.start()
 
-    def w_load(j):
-        rows = pl.ds(pl.multiple_of(j * WIDE, WIDE), WIDE)
-        return pltpu.make_async_copy(w_h.at[rows], w.at[rows], w_sem.at[j])
-
-    @pl.loop(0, NCH)
-    def _(j):
-        w_load(j).start()
+    def w_load(i):
+        rows = pl.ds(pl.multiple_of(i * (DIM // WLOADS), DIM // WLOADS), DIM // WLOADS)
+        return pltpu.make_async_copy(w_h.at[rows], w.at[rows], w_sem.at[i])
+
+    @pl.loop(0, WLOADS)
+    def _(i):
+        w_load(i).start()
 
     xf[0:8, :] = jnp.zeros((8, CHAN), F32)
     tacc[...] = jnp.zeros_like(tacc)
@@ -163,13 +192,9 @@
     def _(i):
         pass_one(i)
 
-    @pl.loop(1, last)
-    def _(i):
-        pass_two(i)
-
     pl.semaphore_wait(
         barrier,
-        NPLANE - 1 + 2 * NEAR + jnp.where(far_next, 1, 0) + jnp.where(far_prev, 1, 0),
+        AROUND + 2 * NEAR + jnp.where(chip_next, 1, 0) + jnp.where(chip_prev, 1, 0),
     )
     for step in (NEAR, NZ - NEAR):
         pl.semaphore_signal(far.at[0], 1, device_id=z_device(z + step), device_id_type=MESH)
@@ -189,6 +214,24 @@
         for copy in to_prev:
             copy.start()
 
+    plane_neighbours(lambda device: pl.semaphore_signal(far.at[2], 1, device_id=device, device_id_type=MESH))
+
+    @pl.loop(1, last)
+    def _(i):
+        pass_two(i)
+
+    loads[4].wait()
+    loads[5].wait()
+
+    def squares(j, total):
+        cols = pl.ds(pl.multiple_of(j * WIDE, WIDE), WIDE)
+        h = hid[:, cols].astype(F32)
+        h = h * h
+        return total + sum(h[:, i * 128 : (i + 1) * 128] for i in range(PER))
+
+    square = lax.fori_loop(0, NCH, squares, jnp.zeros((OWN, 128), F32))
+    rms = jnp.sqrt(jnp.sum(square, -1, keepdims=True) * (1.0 / DIM) + 1e-05)
+    inv[...] = jnp.broadcast_to(1.0 / rms, (OWN, 128))
     pl.semaphore_wait(far.at[0], 2)
     for step in (2 * NEAR, NZ - 2 * NEAR):
         pl.semaphore_signal(far.at[1], 1, device_id=z_device(z + step), device_id_type=MESH)
@@ -217,7 +260,11 @@
 
     def product(j):
         rows = pl.ds(pl.multiple_of(j * WIDE, WIDE), WIDE)
-        w_load(j).wait()
+
+        @pl.when(rem(j, NCH // WLOADS) == 0)
+        def _():
+            w_load(j // (NCH // WLOADS)).wait()
+
         part = lax.dot_general(ing[...], w[rows, :], (((1,), (1,)), ((), ())), preferred_element_type=F32)
         pbuf[j] = part.astype(BF16)
 
@@ -226,7 +273,7 @@
         return remote(
             pbuf.at[j, pl.ds(pl.multiple_of(to * PAIR, PAIR), PAIR)],
             ybuf.at[j, y],
-            ys_sem.at[j],
+            ys_sem,
             yr_sem.at[j],
             {"y": to},
         )
@@ -251,7 +298,7 @@
 
 
     def z_copy(j):
-        return remote(zs.at[j], zr.at[j], zs_sem.at[j], zr_sem.at[j], {"zh": 1 - zh})
+        return remote(zs.at[j], zr.at[j], zs_sem, zr_sem.at[j], {"zh": 1 - zh})
 
     mine = pl.multiple_of(zh * OWN, OWN)
     other = pl.multiple_of((1 - zh) * OWN, OWN)
@@ -262,31 +309,45 @@
 
     def gain_of(j):
         return gain[0:1, pl.ds(pl.multiple_of(j * WIDE, WIDE), WIDE)]
+
+    def share(j, sums):
+        for i in range(PER):
+            gbuf[j, i : i + 1, :] = sums[:, i * 128 : (i + 1) * 128]
+
+    def share_send(j):
+        mine = jnp.logical_and(j == place, owner)
+
+        @pl.when(jnp.logical_not(mine))
+        def _():
+            remote(
+                gbuf.at[j, pl.ds(0, PER)],
+                gr.at[q, pl.ds(0, PER)],
+                small_s.at[2],
+                small_r.at[2],
+                chip_at(j, NC - 1),
+            ).start()
+
+        @pl.when(mine)
+        def _():
+            gr[q, 0:PER, :] = gbuf[j, 0:PER, :]
 
     def arrive(j):
         z_copy(j).wait_recv()
         normed = own[j] + zr[j].astype(F32)
         own[j] = normed
         both = normed * xhat_of(j)
-        sums = jnp.sum(both, 0, keepdims=True)
-        for i in range(PER):
-            gbuf[j * PER + i, 0:1, :] = sums[:, i * 128 : (i + 1) * 128]
+        share(j, jnp.sum(both, 0, keepdims=True))
         both = both * gain_of(j)
         mean[...] += sum(both[:, i * 128 : (i + 1) * 128] for i in range(PER))
-
-        @pl.loop(0, PER)
-        def _(i):
-            p = j * PER + i
-
-            @pl.when(p != q)
-            def _():
-                remote(
-                    gbuf.at[p, pl.ds(0, 1)], gr.at[q, pl.ds(0, 1)], small_s.at[2], small_r.at[2], plane_device(p)
-                ).start()
-
-            @pl.when(p == q)
-            def _():
-                gr[q, 0:1, :] = gbuf[p, 0:1, :]
+        share_send(j)
+
+        @pl.when(j == 3)
+        def _():
+            near_sums()
+
+        @pl.when(j == 10)
+        def _():
+            far_sums()
 
     def forward(j):
         drain(ybuf.at[j, pl.ds(0, NY - 1)], yr_sem.at[j])
@@ -310,9 +371,8 @@
         def _():
             produce(j + FIRST)
 
-    @pl.loop(FIRST + WINDOW, NCH)
-    def _(j):
-        produce(j)
+    pl.semaphore_wait(far.at[2], AROUND)
+    plane_neighbours(lambda device: pl.semaphore_signal(far.at[3], 1, device_id=device, device_id_type=MESH))
 
     sums = [jnp.sum(tacc[k], 0, keepdims=True) for k in range(5)]
     for p in range(NLINE):
@@ -320,19 +380,6 @@
             tpc[p, k : k + 1, :] = sums[k][:, p * 128 : (p + 1) * 128]
     tr[line, 0:5, :] = tpc[line, 0:5, :]
 
-    loads[4].wait()
-    loads[5].wait()
-
-    def squares(j, total):
-        cols = pl.ds(pl.multiple_of(j * WIDE, WIDE), WIDE)
-        h = hid[:, cols].astype(F32)
-        h = h * h
-        return total + sum(h[:, i * 128 : (i + 1) * 128] for i in range(PER))
-
-    square = lax.fori_loop(0, NCH, squares, jnp.zeros((OWN, 128), F32))
-    rms = jnp.sqrt(jnp.sum(square, -1, keepdims=True) * (1.0 / DIM) + 1e-05)
-    inv[...] = jnp.broadcast_to(1.0 / rms, (OWN, 128))
-
     def line_copy(k, src, dst, i):
         return remote(src, dst, small_s.at[i], small_r.at[i], line_device(rem(line + k, NLINE)))
 
@@ -365,38 +412,32 @@
         def _(k):
             far_copy(k).start()
 
+    pl.semaphore_wait(far.at[3], AROUND)
+
     @pl.loop(WINDOW, NCH)
     def _(j):
         forward(j)
-
         arrive(j - WINDOW)
-
-        @pl.when(j == NCH - 4)
-        def _():
-            near_sums()
-
-        @pl.when(j == NCH - 1)
-        def _():
-            far_sums()
 
     @pl.loop(NCH - WINDOW, NCH)
     def _(j):
         arrive(j)
 
-    drain(gr.at[pl.ds(0, NPLANE - 1), pl.ds(0, 1)], small_r.at[2])
-    za[z, 0:1, :] = jnp.sum(gr[:, 0:1, :], 0)
-
-    def z_share(k):
-        remote(
-            za.at[z, pl.ds(0, 1)], za.at[z, pl.ds(0, 1)], small_s.at[4], small_r.at[4], z_device(z + k)
-        ).start()
-
-    z_share(NZ // 2)
-
-    @pl.loop(1, NZ // 2)
-    def _(k):
-        z_share(NZ // 2 - k)
-        z_share(NZ // 2 + k)
+    @pl.when(owner)
+    def _():
+        drain(gr.at[pl.ds(0, NPLANE - 1), pl.ds(0, PER)], small_r.at[2])
+        za[z, 0:PER, :] = jnp.sum(gr[:, 0:PER, :], 0)
+
+        def z_share(k):
+            mine = za.at[z, pl.ds(0, PER)]
+            remote(mine, mine, small_s.at[4], small_r.at[4], z_device(z + k)).start()
+
+        z_share(NZ // 2)
+
+        @pl.loop(1, NZ // 2)
+        def _(k):
+            z_share(NZ // 2 - k)
+            z_share(NZ // 2 + k)
 
     average = jnp.sum(mean[...], -1, keepdims=True) * (1.0 / DIM)
 
@@ -413,14 +454,19 @@
     def _(k):
         line_copy(k, tf.at[line, pl.ds(0, 5)], tf.at[line, pl.ds(0, 5)], 3).start()
 
-    drain(za.at[pl.ds(0, NZ - 1), pl.ds(0, 1)], small_r.at[4])
-    ga[q, 0:1, :] = jnp.sum(za[:, 0:1, :], 0)
-
-    @pl.loop(1, NPLANE)
-    def _(k):
-        remote(
-            ga.at[q, pl.ds(0, 1)], ga.at[q, pl.ds(0, 1)], small_s.at[5], small_r.at[5], plane_device(rem(q + k, NPLANE))
-        ).start()
+    @pl.when(owner)
+    def _():
+        drain(za.at[pl.ds(0, NZ - 1), pl.ds(0, PER)], small_r.at[4])
+        ga[place, 0:PER, :] = jnp.sum(za[:, 0:PER, :], 0)
+
+        @pl.loop(0, NPLANE)
+        def _(k):
+            to = NPLANE - 1 - k
+
+            @pl.when(to != place * NC + c)
+            def _():
+                mine = ga.at[place, pl.ds(0, PER)]
+                remote(mine, mine, small_s.at[5], small_r.at[5], chip_at(to // NC, rem(to, NC))).start()
 
     drain(tf.at[pl.ds(0, NLINE - 1), pl.ds(0, 5)], small_r.at[3])
     for p in range(NLINE):
@@ -436,20 +482,29 @@
         for copy in to_prev:
             copy.wait_send()
 
-    @pl.loop(0, NCH)
-    def _(j):
-        drain(ybuf.at[j, pl.ds(0, NY - 1)], ys_sem.at[j])
-        z_copy(j).wait_send()
-
+    drain(ybuf.at[:, pl.ds(0, NY - 1)], ys_sem)
+    drain(zs, zs_sem)
     drain(tr.at[pl.ds(0, NLINE - 1), pl.ds(0, 5)], small_s.at[0])
     drain(tn.at[pl.ds(0, GROUP - 1), pl.ds(0, 5)], small_s.at[1])
     drain(tz.at[pl.ds(0, NZL // GROUP - 1), pl.ds(0, 5)], small_s.at[6])
-    drain(gr.at[pl.ds(0, NPLANE - 1), pl.ds(0, 1)], small_s.at[2])
     drain(tf.at[pl.ds(0, NLINE - 1), pl.ds(0, 5)], small_s.at[3])
-    drain(za.at[pl.ds(0, NZ - 1), pl.ds(0, 1)], small_s.at[4])
-    drain(ga.at[pl.ds(0, NPLANE - 1), pl.ds(0, 1)], small_r.at[5])
-    gain_o[...] = ga[:, 0, :]
-    drain(ga.at[pl.ds(0, NPLANE - 1), pl.ds(0, 1)], small_s.at[5])
+
+    @pl.when(owner)
+    def _():
+        drain(gr.at[pl.ds(0, NCH - 1), pl.ds(0, PER)], small_s.at[2])
+        drain(za.at[pl.ds(0, NZ - 1), pl.ds(0, PER)], small_s.at[4])
+        drain(ga.at[pl.ds(0, NCH - 1), pl.ds(0, PER)], small_r.at[5])
+
+    @pl.when(jnp.logical_not(owner))
+    def _():
+        drain(gr.at[pl.ds(0, NCH), pl.ds(0, PER)], small_s.at[2])
+        drain(ga.at[pl.ds(0, NCH), pl.ds(0, PER)], small_r.at[5])
+
+    gain_o[...] = ga[:, 0:PER, :]
+
+    @pl.when(owner)
+    def _():
+        drain(gr.at[pl.ds(0, NPLANE - 1), pl.ds(0, PER)], small_s.at[5])
 
 
 def hand_on(*arrays):
@@ -481,7 +536,7 @@
         kernel,
         out_shape=(
             jax.ShapeDtypeStruct((OWN, DIM), BF16),
-            jax.ShapeDtypeStruct((NPLANE, 128), F32),
+            jax.ShapeDtypeStruct((NCH, PER, 128), F32),
             jax.ShapeDtypeStruct((4, CHAN), F32),
             jax.ShapeDtypeStruct((1, CHAN), F32),
         ),
@@ -509,26 +564,26 @@
             vmem((NCH, OWN, WIDE), BF16),
             vmem((OWN, 128), F32),
             vmem((OWN, 128), F32),
-            vmem((NPLANE, 8, 128), F32),
+            vmem((NCH, 8, 128), F32),
             vmem((NPLANE, 8, 128), F32),
             vmem((NZ, 8, 128), F32),
-            vmem((NPLANE, 8, 128), F32),
+            vmem((NCH, 8, 128), F32),
             vmem((NLINE, 8, 128), F32),
             vmem((NLINE, 8, 128), F32),
             vmem((GROUP, 8, 128), F32),
             vmem((NZL // GROUP, 8, 128), F32),
             vmem((NLINE, 8, 128), F32),
             dma((6,)),
-            dma((NCH,)),
+            dma((WLOADS,)),
             dma((3,)),
             dma((3,)),
+            dma,
             dma((NCH,)),
-            dma((NCH,)),
-            dma((NCH,)),
+            dma,
             dma((NCH,)),
             dma((7,)),
             dma((7,)),
-            pltpu.SemaphoreType.REGULAR((2,)),
+            pltpu.SemaphoreType.REGULAR((4,)),
         ],
         compiler_params=pltpu.CompilerParams(collective_id=0, has_side_effects=True, vmem_limit_bytes=40 << 20),
         name="layer_backward",

time: 109 us -> 104 us (0.954)
  Pallas kernels: 108 us -> 103 us
    pallas_call x1, Pallas kernels: 107 us -> 103 us  [on_device(): pl.pallas_call(kernel, out_shape=(jax.ShapeDtypeStruct((OWN, DIM), BF16),...]
where the time goes in v3:
time: 104 us
  Pallas kernels  103 us (99%)
    pallas_call x1, Pallas kernels, on_device(): pl.pallas_call(kernel, out_shape=(jax.ShapeDtypeStruct((OWN, DIM), BF16),...  103 us

profile of v3, /device:TPU:1, one launch (start us, length us, event | category | flops | bytes accessed | tf_op | source)
XLA Modules:
  0.0 104.0 jit_solution(11103478459962963202)
XLA Ops:
  0.6 102.6 %layer_backward.1 = (bf16[32,4096]{1,0:T(8,128)(2,1)S(1)}, f32[16,2,128]{2,1,0:T(2,128)S(1)}, f32[4,1024]{1,0:T(4,128)S(1)}, f32[1,1024]{1,0:T(1,128)S(1)}) custom-call(bf16[32,4096]{1,0:T(8,128)(2,1)} %hid_h.1, f32[1,4096]{1,0:T(1,128)} %bitcast.4, bf16[4096,1024]{1,0:T(8,128)(2,1)} %w_h.1, bf16[256,1024]{1,0:T(8,128)(2,1)} %conv_h.1, f32[4,1024]{1,0:T(4,128)} %cw_h.1, ...), custom_call_target="tpu_custom_call" | custom-call | tf_op jit(solution)/shard_map/layer_backward/pallas_call | solution.py:535
  103.3 0.7 hand_on.1

commit v4 on v3

--- a/solution.py
+++ b/solution.py
@@ -23,8 +23,9 @@
 TILE = 16
 NEAR = 4
 AROUND = NY - 1 + NX - 1 + NC - 1
-WINDOW = 8
-FIRST = 10
+WINDOW = 9
+FIRST = 7
+EXTRA = 3
 WLOADS = 4
 GROUP = 4
 F32 = jnp.float32
@@ -86,6 +87,7 @@
     line = x * NC + c
     place = sum(jnp.where(jnp.logical_and(x == a, y == b), i, 0) for i, (a, b) in enumerate(CHIPS))
     owner = c == NC - 1
+    ahead = WINDOW + EXTRA * (1 - c)
     n = zl * NLINE + line
     has_next = n < NCTX - 1
     has_prev = n > 0
@@ -363,7 +365,7 @@
     mean[...] = jnp.zeros_like(mean)
     pl.semaphore_wait(far.at[1], 2)
 
-    @pl.loop(0, WINDOW)
+    @pl.loop(0, ahead)
     def _(j):
         forward(j)
 
@@ -414,12 +416,12 @@
 
     pl.semaphore_wait(far.at[3], AROUND)
 
-    @pl.loop(WINDOW, NCH)
+    @pl.loop(ahead, NCH)
     def _(j):
         forward(j)
-        arrive(j - WINDOW)
-
-    @pl.loop(NCH - WINDOW, NCH)
+        arrive(j - ahead)
+
+    @pl.loop(NCH - ahead, NCH)
     def _(j):
         arrive(j)
 

time: 104 us -> 104 us (level)
  no operation moved by 1% of the time
where the time goes in v4:
time: 104 us
  Pallas kernels  103 us (99%)
    pallas_call x1, Pallas kernels, on_device(): pl.pallas_call(kernel, out_shape=(jax.ShapeDtypeStruct((OWN, DIM), BF16),...  102 us

profile of v4, /device:TPU:1, one launch (start us, length us, event | category | flops | bytes accessed | tf_op | source)
XLA Modules:
  0.0 103.6 jit_solution(11027751516053201107)
XLA Ops:
  0.6 102.2 %layer_backward.1 = (bf16[32,4096]{1,0:T(8,128)(2,1)S(1)}, f32[16,2,128]{2,1,0:T(2,128)S(1)}, f32[4,1024]{1,0:T(4,128)S(1)}, f32[1,1024]{1,0:T(1,128)S(1)}) custom-call(bf16[32,4096]{1,0:T(8,128)(2,1)} %hid_h.1, f32[1,4096]{1,0:T(1,128)} %bitcast.4, bf16[4096,1024]{1,0:T(8,128)(2,1)} %w_h.1, bf16[256,1024]{1,0:T(8,128)(2,1)} %conv_h.1, f32[4,1024]{1,0:T(4,128)} %cw_h.1, ...), custom_call_target="tpu_custom_call" | custom-call | tf_op jit(solution)/shard_map/layer_backward/pallas_call | solution.py:537
  102.9 0.7 hand_on.1

commit v5 on v4

--- a/solution.py
+++ b/solution.py
@@ -436,8 +436,7 @@
 
         z_share(NZ // 2)
 
-        @pl.loop(1, NZ // 2)
-        def _(k):
+        for k in range(1, NZ // 2):
             z_share(NZ // 2 - k)
             z_share(NZ // 2 + k)
 
@@ -455,20 +454,6 @@
     @pl.loop(1, NLINE)
     def _(k):
         line_copy(k, tf.at[line, pl.ds(0, 5)], tf.at[line, pl.ds(0, 5)], 3).start()
-
-    @pl.when(owner)
-    def _():
-        drain(za.at[pl.ds(0, NZ - 1), pl.ds(0, PER)], small_r.at[4])
-        ga[place, 0:PER, :] = jnp.sum(za[:, 0:PER, :], 0)
-
-        @pl.loop(0, NPLANE)
-        def _(k):
-            to = NPLANE - 1 - k
-
-            @pl.when(to != place * NC + c)
-            def _():
-                mine = ga.at[place, pl.ds(0, PER)]
-                remote(mine, mine, small_s.at[5], small_r.at[5], chip_at(to // NC, rem(to, NC))).start()
 
     drain(tf.at[pl.ds(0, NLINE - 1), pl.ds(0, 5)], small_r.at[3])
     for p in range(NLINE):
@@ -495,11 +480,32 @@
     def _():
         drain(gr.at[pl.ds(0, NCH - 1), pl.ds(0, PER)], small_s.at[2])
         drain(za.at[pl.ds(0, NZ - 1), pl.ds(0, PER)], small_s.at[4])
+
+    @pl.when(jnp.logical_not(owner))
+    def _():
+        drain(gr.at[pl.ds(0, NCH), pl.ds(0, PER)], small_s.at[2])
+
+    @pl.when(owner)
+    def _():
+        drain(za.at[pl.ds(0, NZ - 1), pl.ds(0, PER)], small_r.at[4])
+        ga[place, 0:PER, :] = jnp.sum(za[:, 0:PER, :], 0)
+
+        mine = ga.at[place, pl.ds(0, PER)]
+        for i, j in reversed(CHIPS):
+            for core in reversed(range(NC)):
+                here = (x == i) & (y == j) & (c == core)
+
+                @pl.when(jnp.logical_not(here))
+                def _():
+                    to = {"x": i, "y": j, "c": core}
+                    remote(mine, mine, small_s.at[5], small_r.at[5], to).start()
+
+    @pl.when(owner)
+    def _():
         drain(ga.at[pl.ds(0, NCH - 1), pl.ds(0, PER)], small_r.at[5])
 
     @pl.when(jnp.logical_not(owner))
     def _():
-        drain(gr.at[pl.ds(0, NCH), pl.ds(0, PER)], small_s.at[2])
         drain(ga.at[pl.ds(0, NCH), pl.ds(0, PER)], small_r.at[5])
 
     gain_o[...] = ga[:, 0:PER, :]

time: 104 us -> 104 us (level)
  no operation moved by 1% of the time
where the time goes in v5:
time: 104 us; the launch traced here: 103 us
  Pallas kernels  103 us (99%)
    pallas_call x1, Pallas kernels, on_device(): pl.pallas_call(kernel, out_shape=(jax.ShapeDtypeStruct((OWN, DIM), BF16),...  102 us

profile of v5, /device:TPU:1, one launch (start us, length us, event | category | flops | bytes accessed | tf_op | source)
XLA Modules:
  0.0 103.4 jit_solution(18261254981333572831)
XLA Ops:
  0.6 102.0 %layer_backward.1 = (bf16[32,4096]{1,0:T(8,128)(2,1)S(1)}, f32[16,2,128]{2,1,0:T(2,128)S(1)}, f32[4,1024]{1,0:T(4,128)S(1)}, f32[1,1024]{1,0:T(1,128)S(1)}) custom-call(bf16[32,4096]{1,0:T(8,128)(2,1)} %hid_h.1, f32[1,4096]{1,0:T(1,128)} %bitcast.4, bf16[4096,1024]{1,0:T(8,128)(2,1)} %w_h.1, bf16[256,1024]{1,0:T(8,128)(2,1)} %conv_h.1, f32[4,1024]{1,0:T(4,128)} %cw_h.1, ...), custom_call_target="tpu_custom_call" | custom-call | tf_op jit(solution)/shard_map/layer_backward/pallas_call | solution.py:543
  102.6 0.7 hand_on.1

commit v6 on v5

--- a/solution.py
+++ b/solution.py
@@ -362,6 +362,9 @@
         own[j] = total(mine)
         z_copy(j).start()
 
+    pl.semaphore_wait(far.at[2], AROUND)
+    plane_neighbours(lambda device: pl.semaphore_signal(far.at[3], 1, device_id=device, device_id_type=MESH))
+
     mean[...] = jnp.zeros_like(mean)
     pl.semaphore_wait(far.at[1], 2)
 
@@ -373,8 +376,6 @@
         def _():
             produce(j + FIRST)
 
-    pl.semaphore_wait(far.at[2], AROUND)
-    plane_neighbours(lambda device: pl.semaphore_signal(far.at[3], 1, device_id=device, device_id_type=MESH))
 
     sums = [jnp.sum(tacc[k], 0, keepdims=True) for k in range(5)]
     for p in range(NLINE):
@@ -434,11 +435,19 @@
             mine = za.at[z, pl.ds(0, PER)]
             remote(mine, mine, small_s.at[4], small_r.at[4], z_device(z + k)).start()
 
-        z_share(NZ // 2)
-
+        @pl.when(z != 0)
+        def _():
+            z_share(NZ - z)
+
+        def z_other(k):
+            @pl.when(rem(z + k, NZ) != 0)
+            def _():
+                z_share(k)
+
+        z_other(NZ // 2)
         for k in range(1, NZ // 2):
-            z_share(NZ // 2 - k)
-            z_share(NZ // 2 + k)
+            z_other(NZ // 2 - k)
+            z_other(NZ // 2 + k)
 
     average = jnp.sum(mean[...], -1, keepdims=True) * (1.0 / DIM)
 

time: 104 us -> 103 us (level)
  no operation moved by 1% of the time
where the time goes in v6:
time: 103 us
  Pallas kernels  103 us (100%)
    pallas_call x1, Pallas kernels, on_device(): pl.pallas_call(kernel, out_shape=(jax.ShapeDtypeStruct((OWN, DIM), BF16),...  102 us

profile of v6, /device:TPU:1, one launch (start us, length us, event | category | flops | bytes accessed | tf_op | source)
XLA Modules:
  0.0 103.3 jit_solution(13040585419946350988)
XLA Ops:
  0.6 102.0 %layer_backward.1 = (bf16[32,4096]{1,0:T(8,128)(2,1)S(1)}, f32[16,2,128]{2,1,0:T(2,128)S(1)}, f32[4,1024]{1,0:T(4,128)S(1)}, f32[1,1024]{1,0:T(1,128)S(1)}) custom-call(bf16[32,4096]{1,0:T(8,128)(2,1)} %hid_h.1, f32[1,4096]{1,0:T(1,128)} %bitcast.4, bf16[4096,1024]{1,0:T(8,128)(2,1)} %w_h.1, bf16[256,1024]{1,0:T(8,128)(2,1)} %conv_h.1, f32[4,1024]{1,0:T(4,128)} %cw_h.1, ...), custom_call_target="tpu_custom_call" | custom-call | tf_op jit(solution)/shard_map/layer_backward/pallas_call | solution.py:552
  102.6 0.7 hand_on.1
